TPU v7x, 32 devices: a whole 2x2x4 slice. The times are simulated.
32 devices in a mesh: grp: 2 (over y), shard: 8 (over z, x), rep: 2 (over core).
Axes of the slice: x: 2, y: 2, z: 4, core: 2. Of those that a mesh axis runs over, the one named last changes fastest.
Arguments:
- replica_weights: bfloat16 [4, 4096, 14336], P(('grp', 'rep'), None, 'shard'), parts along dimension 0, may hold values from -6 to 6
- global_weights: float32 [8192, 14336], P(('grp', 'shard', 'rep')), parts along dimension 0, may hold values from -6 to 6
- momentum: float32 [8192, 14336], P(('grp', 'shard', 'rep')), parts along dimension 0, may hold values from -3 to 3
Outputs:
- new_params: bfloat16 [8192, 14336], P('grp', 'shard'), parts along dimension 0
- new_global: float32 [8192, 14336], P(('grp', 'shard', 'rep')), parts along dimension 0
- new_momentum: float32 [8192, 14336], P(('grp', 'shard', 'rep')), parts along dimension 0
There are 2 independent parts, one for each index of `grp`. A program takes and returns all parts, laid end to end along the dimension named above; each array names one. Nothing has to cross between parts.
All inputs are finite; a program needn't handle non-finite values.
Results may differ from a plain program's by a relative error of at most 0.008.
Values may be sent and summed in bfloat16 or wider, within the bound.
A program may use at most 192 MiB of HBM per device.

v0:
```python
import jax
import jax.numpy as jnp
from jax import lax
from jax.sharding import PartitionSpec as P

outer_rate = 0.7
momentum_decay = 0.9


def on_device(replica_weights, global_weights, momentum):
    local = replica_weights[0]
    rows, width = local.shape
    shards = lax.axis_size("shard")
    pairs = lax.axis_size("rep")
    owned = global_weights.shape[0]
    block = lax.all_to_all(local, "shard", split_axis=0, concat_axis=1, tiled=True)
    total = lax.psum_scatter(
        block.astype(jnp.float32).astype(jnp.bfloat16), "rep", scatter_dimension=0, tiled=True
    ).astype(jnp.float32)
    delta = global_weights - total / jnp.float32(pairs)
    new_momentum = momentum_decay * momentum + delta
    new_global = global_weights - outer_rate * (delta + momentum_decay * new_momentum)
    fresh = new_global.astype(jnp.bfloat16)
    spread = lax.all_to_all(fresh, "shard", split_axis=1, concat_axis=0, tiled=True)
    whole = lax.all_gather(
        spread.reshape(shards, 1, owned, width), "rep", axis=1, tiled=True
    ).reshape(rows, width)
    return (whole, new_global, new_momentum)


def solution(mesh):
    placed = (
        P(("grp", "rep"), None, "shard"),
        P(("grp", "shard", "rep"), None),
        P(("grp", "shard", "rep"), None),
    )
    return jax.shard_map(
        on_device,
        mesh=mesh,
        in_specs=placed,
        out_specs=(
            P("grp", "shard"),
            P(("grp", "shard", "rep"), None),
            P(("grp", "shard", "rep"), None),
        ),
        check_vma=False,
    )
```

profile of v0, /device:TPU:10, one launch (start us, length us, event | category | flops | bytes accessed | tf_op | source)
XLA Modules:
  0.0 638.4 jit_solution(7840388707112944055)
XLA Ops:
  7.2 0.0 reduce-scatter.2.cloned.1.call-start
  7.2 323.6 %all_to_all.35 = bf16[8,512,1792]{2,1,0:T(8,128)(2,1)} all-to-all(bf16[8,512,1792]{2,1,0:T(8,128)(2,1)} %bitcast.10), channel_id=1, replica_groups=mesh['grp'=2,'shard'=8,'rep'=2] {'shard'}, dimensions={0} | all-to-all | bytes 29360128 | tf_op jit(solution)/shard_map/all_to_all | solution.py:16
  330.9 18.7 %copy.9 = bf16[8,512,1792]{1,2,0:T(8,128)(2,1)} copy(bf16[8,512,1792]{2,1,0:T(8,128)(2,1)} %all_to_all.35) | data formatting | bytes 29360128 | tf_op jit(solution)/shard_map/all_to_all | solution.py:16
  349.5 0.0 reduce-scatter.2.cloned.1.call-update
  349.6 0.0 all-gather.3.cloned.1.call-start
  349.6 15.9 %copy.12 = f32[256,14336]{0,1:T(8,128)} copy(f32[256,14336]{1,0:T(8,128)} %param.4) | data formatting | bytes 29360128 | tf_op args[1]
  365.5 14.9 %copy.11 = f32[256,14336]{0,1:T(8,128)} copy(f32[256,14336]{1,0:T(8,128)} %param.5) | data formatting | bytes 29360128 | tf_op args[2]
  380.4 0.0 reduce-scatter.2.cloned.1.call-done
  380.4 23.2 %fusion = (bf16[256,14336]{0,1:T(8,128)(2,1)}, f32[256,14336]{0,1:T(8,128)}, f32[256,14336]{0,1:T(8,128)}) fusion(f32[256,14336]{0,1:T(8,128)} %copy.12, f32[256,14336]{0,1:T(8,128)} %copy.11, bf16[256,14336]{0,1:T(8,128)(2,1)} %reduce-scatter.2.cloned.1.call-done), kind=kLoop, calls=%fused_computation.3 | loop fusion | flops 36700160 | bytes 73400320 | tf_op jit(solution)/shard_map/convert_element_type | solution.py:23
  403.6 9.9 %copy.13 = bf16[256,8,1792]{2,0,1:T(8,128)(2,1)} copy(bf16[256,8,1792]{0,2,1:T(8,128)(2,1)} %bitcast.8) | data formatting | bytes 14680064 | tf_op jit(solution)/shard_map/all_to_all | solution.py:24
  413.5 165.3 %all_to_all.36 = bf16[256,8,1792]{2,0,1:T(8,128)(2,1)S(1)} all-to-all(bf16[256,8,1792]{2,0,1:T(8,128)(2,1)} %copy.13), channel_id=1, replica_groups=mesh['grp'=2,'shard'=8,'rep'=2] {'shard'}, dimensions={1} | all-to-all | bytes 14680064 | tf_op jit(solution)/shard_map/all_to_all | solution.py:24
  578.8 7.0 %copy.14 = bf16[8,256,1792]{2,0,1:T(8,128)(2,1)} copy(bf16[8,256,1792]{2,1,0:T(8,128)(2,1)S(1)} %bitcast.9) | data formatting | bytes 14680064 | tf_op jit(solution)/shard_map/all_to_all | solution.py:24
  585.7 0.0 all-gather.3.cloned.1.call-update
  585.8 15.6 %copy.16 = f32[256,14336]{1,0:T(8,128)} copy(f32[256,14336]{0,1:T(8,128)} %get-tuple-element.7) | data formatting | bytes 29360128
  601.4 15.5 %copy.17 = f32[256,14336]{1,0:T(8,128)} copy(f32[256,14336]{0,1:T(8,128)} %get-tuple-element.8) | data formatting | bytes 29360128
  616.9 0.0 all-gather.3.cloned.1.call-done
  616.9 14.7 %copy.15 = bf16[8,512,1792]{2,1,0:T(8,128)(2,1)} copy(bf16[8,512,1792]{2,0,1:T(8,128)(2,1)} %all-gather.3.cloned.1.call-done) | data formatting | bytes 29360128 | tf_op jit(solution)/shard_map/all_gather | solution.py:25
Async XLA Ops:
  7.2 373.2 %reduce-scatter.2.cloned.1.call-start = ((), (), s32[]{:S(2)}) async-start(), calls=%async_computation.3 | async-start | bytes 22020096 | tf_op jit(solution)/shard_map/reduce_scatter | solution.py:17
  349.6 267.3 %all-gather.3.cloned.1.call-start = ((), (), s32[]{:S(2)}) async-start(), calls=%async_computation.4 | async-start | bytes 22020096 | tf_op jit(solution)/shard_map/all_gather | solution.py:25
Sparse Core Ops, SparseCore 0:
  349.7 21.9 reduce-scatter.1
  585.9 27.8 all-gather.2
where the time goes:
time: 644 us; the launch traced here: 638 us
  blocking collectives  489 us (76%)
  local copies, waits for them, and re-layouts  112 us (17%)
  other arithmetic  23.2 us (4%)
  between operations  14 us (2%)
    all_to_all x1, blocking collectives, on_device(): lax.all_to_all(local, 'shard', split_axis=0, concat_axis=1, tiled=True)  324 us
    all_to_all x1, blocking collectives, on_device(): lax.all_to_all(fresh, 'shard', split_axis=1, concat_axis=0, tiled=True)  165 us
    unnamed x4, local copies, waits for them, and re-layouts  61.9 us
    convert_element_type x1, other arithmetic, on_device(): fresh = new_global.astype(jnp.bfloat16)  23.2 us
    all_to_all x1, local copies, waits for them, and re-layouts, on_device(): lax.all_to_all(local, 'shard', split_axis=0, concat_axis=1, tiled=True)  18.7 us
    all_to_all x2, local copies, waits for them, and re-layouts, on_device(): lax.all_to_all(fresh, 'shard', split_axis=1, concat_axis=0, tiled=True)  16.9 us
    all_gather x1, local copies, waits for them, and re-layouts, on_device(): lax.all_gather(spread.reshape(shards, 1, owned, width), 'rep', axis=1, ti...  14.7 us
  transfers between devices with their start and end apart: 2, of which 0 were waited for; matrix products, arithmetic and copies ran while one was open for 10% of the time, Pallas kernels for 0%

commit v1 on v0

v1 whole, which is shorter than its diff:
```python
import functools

import jax
import jax.numpy as jnp
from jax import lax
from jax.experimental import pallas as pl
from jax.experimental.pallas import tpu as pltpu
from jax.sharding import PartitionSpec as P

outer_rate = 0.7
momentum_decay = 0.9
LANES = 128
CHUNK = 16


def far_first(n):
    return sorted(range(1, n), key=lambda k: abs(2 * k - n)) + [0]


def exchange(n, pairs, w_ref, g_ref, m_ref, t_ref, p_ref, peer_w, tot, q_out, q_in,
             g_buf, m_buf, w_buf, load_g, load_m, load_w, w_send, w_recv,
             q_send, q_recv, t_send, t_recv, p_send, p_recv, p_local, t_local):
    me, rep = lax.axis_index("shard"), lax.axis_index("rep")
    other = 1 - rep
    owned, width = g_buf.shape[1:]
    steps = far_first(n)
    on_total = outer_rate * (1 + momentum_decay) / pairs
    on_global = 1 - outer_rate * (1 + momentum_decay)
    on_momentum = -outer_rate * momentum_decay * momentum_decay

    def ahead(k):
        return lax.rem(me + k, n)

    def columns(shard):
        return pl.ds(pl.multiple_of(shard * width, LANES), width)

    def rows(shard, which):
        return pl.ds(pl.multiple_of((shard * pairs + which) * owned, CHUNK), owned)

    def chunks(body):
        def one(j, carry):
            body(pl.ds(pl.multiple_of(j * CHUNK, CHUNK), CHUNK))
            return carry
        lax.fori_loop(0, owned // CHUNK, one, 0)

    def remote(src, dst, send, recv, to):
        return pltpu.make_async_remote_copy(
            src_ref=src, dst_ref=dst, send_sem=send, recv_sem=recv,
            device_id=to, device_id_type=pl.DeviceIdType.MESH)

    def outer_loads(i):
        cols = columns(ahead(steps[i]))
        return (pltpu.make_async_copy(g_ref.at[:, cols], g_buf.at[i % 2], load_g.at[i % 2]),
                pltpu.make_async_copy(m_ref.at[:, cols], m_buf.at[i % 2], load_m.at[i % 2]))

    def weight_load(i):
        return pltpu.make_async_copy(
            w_ref.at[rows(ahead(steps[i]), rep)], w_buf.at[i % 2], load_w.at[i % 2])

    for copy in outer_loads(0):
        copy.start()
    weight_load(0).start()

    barrier = pltpu.get_barrier_semaphore()
    for k in steps[:-1]:
        pl.semaphore_signal(barrier, inc=1, device_id={"shard": ahead(k)},
                            device_id_type=pl.DeviceIdType.MESH)
    pl.semaphore_signal(barrier, inc=1, device_id={"rep": other},
                        device_id_type=pl.DeviceIdType.MESH)
    pl.semaphore_wait(barrier, n)

    w_copies, q_copies, t_copies, p_copies, locals_ = [], [], [], [], []
    for i, k in enumerate(steps):
        copy = remote(w_ref.at[rows(ahead(k), other)], peer_w.at[i],
                      w_send.at[i], w_recv.at[i], {"rep": other})
        copy.start()
        w_copies.append(copy)

    for i, k in enumerate(steps):
        if i + 1 < n:
            for copy in outer_loads(i + 1):
                copy.start()
        for copy in outer_loads(i):
            copy.wait()
        out = q_out.at[i] if k else q_in.at[i]

        def state_term(at, i=i, out=out):
            out[at, :] = (on_global * g_buf[i % 2, at, :]
                          + on_momentum * m_buf[i % 2, at, :]).astype(out.dtype)
        chunks(state_term)
        if k:
            copy = remote(q_out.at[i], q_in.at[i], q_send.at[i], q_recv.at[i],
                          {"shard": ahead(k)})
            copy.start()
            q_copies.append(copy)

    for i, k in enumerate(steps):
        if i + 1 < n:
            weight_load(i + 1).start()
        weight_load(i).wait()
        w_copies[i].wait_recv()

        def add(at, i=i):
            tot[i, at, :] = (w_buf[i % 2, at, :].astype(jnp.float32)
                             + peer_w[i, at, :].astype(jnp.float32)).astype(tot.dtype)
        chunks(add)
        if k:
            copy = remote(tot.at[i], t_ref.at[:, columns(me)], t_send.at[i], t_recv.at[i],
                          {"shard": ahead(k)})
            t_copies.append(copy)
        else:
            copy = pltpu.make_async_copy(tot.at[i], t_ref.at[:, columns(me)], t_local)
            locals_.append(copy)
        copy.start()

    for j in [n - 1] + list(range(n - 1)):
        k = steps[j]
        i = steps.index((n - k) % n)
        if k:
            q_copies[j].wait_recv()

        def weights(at, i=i, j=j):
            q_in[j, at, :] = (q_in[j, at, :].astype(jnp.float32)
                              + on_total * tot[i, at, :].astype(jnp.float32)).astype(q_in.dtype)
        chunks(weights)
        target = p_ref.at[rows(ahead((n - k) % n), rep)]
        copy = remote(q_in.at[j], target, p_send.at[j], p_recv.at[j], {"rep": other})
        copy.start()
        p_copies.append(copy)
        copy = pltpu.make_async_copy(q_in.at[j], target, p_local.at[j])
        copy.start()
        locals_.append(copy)

    for copy in w_copies + q_copies:
        copy.wait_send()
    for copy in p_copies + t_copies:
        copy.wait()
    for copy in locals_:
        copy.wait()


def by_kernel(local, global_weights, momentum, n, pairs):
    owned = global_weights.shape[0]
    rows, width = local.shape
    anywhere = pl.BlockSpec(memory_space=pl.ANY)
    block = (owned, width)
    dma = pltpu.SemaphoreType.DMA
    return pl.pallas_call(
        functools.partial(exchange, n, pairs),
        out_shape=(jax.ShapeDtypeStruct((owned, n * width), jnp.bfloat16),
                   jax.ShapeDtypeStruct((rows, width), jnp.bfloat16)),
        in_specs=[anywhere] * 3,
        out_specs=(anywhere, anywhere),
        scratch_shapes=[pltpu.VMEM((n,) + block, jnp.bfloat16)] * 4
        + [pltpu.VMEM((2,) + block, jnp.float32)] * 2
        + [pltpu.VMEM((2,) + block, jnp.bfloat16)]
        + [dma((2,))] * 3 + [dma((n,))] * 9 + [dma],
        compiler_params=pltpu.CompilerParams(
            collective_id=0, has_side_effects=True, vmem_limit_bytes=60 * 2**20),
    )(local, global_weights, momentum)


def by_collectives(local, global_weights, momentum, n, pairs):
    owned = global_weights.shape[0]
    rows, width = local.shape
    halves = lax.psum_scatter(local.reshape(n, pairs, owned, width), "rep",
                              scatter_dimension=1, tiled=True).reshape(n * owned, width)
    total = lax.all_to_all(halves, "shard", split_axis=0, concat_axis=1, tiled=True)
    return total


def on_device(replica_weights, global_weights, momentum):
    local = replica_weights[0]
    rows, width = local.shape
    n, pairs = lax.axis_size("shard"), lax.axis_size("rep")
    owned = global_weights.shape[0]
    kernel = pairs == 2 and n > 1 and width % LANES == 0 and owned % CHUNK == 0
    whole = None
    if kernel:
        total, whole = by_kernel(local, global_weights, momentum, n, pairs)
    else:
        total = by_collectives(local, global_weights, momentum, n, pairs)
    delta = global_weights - total.astype(jnp.float32) / jnp.float32(pairs)
    new_momentum = momentum_decay * momentum + delta
    new_global = global_weights - outer_rate * (delta + momentum_decay * new_momentum)
    if not kernel:
        fresh = new_global.astype(jnp.bfloat16)
        spread = lax.all_to_all(fresh, "shard", split_axis=1, concat_axis=0, tiled=True)
        whole = lax.all_gather(
            spread.reshape(n, 1, owned, width), "rep", axis=1, tiled=True
        ).reshape(rows, width)
    return (whole, new_global, new_momentum)


def solution(mesh):
    placed = (
        P(("grp", "rep"), None, "shard"),
        P(("grp", "shard", "rep"), None),
        P(("grp", "shard", "rep"), None),
    )
    return jax.shard_map(
        on_device,
        mesh=mesh,
        in_specs=placed,
        out_specs=(
            P("grp", "shard"),
            P(("grp", "shard", "rep"), None),
            P(("grp", "shard", "rep"), None),
        ),
        check_vma=False,
    )
```

time: 644 us -> 353 us (0.55)
  blocking collectives: 489 us -> 0 us
  Pallas kernels: 0 us -> 320 us
  local copies, waits for them, and re-layouts: 112 us -> 8.77 us
  between operations: 14 us -> 0.65 us
    all_to_all x2 -> x0, blocking collectives: 489 us -> none  [the longest x1 324 us: on_device(): lax.all_to_all(local, 'shard', split_axis=0, concat_axis=1, tiled=True)]
    pallas_call x0 -> x1, Pallas kernels: none -> 320 us  [by_kernel(): pl.pallas_call(functools.partial(exchange, n, pairs), out_shape=(jax.Shap...]
    unnamed x4 -> x3, local copies, waits for them, and re-layouts: 61.9 us -> 8.77 us
    all_to_all x3 -> x0, local copies, waits for them, and re-layouts: 35.6 us -> none  [the longest x1 18.7 us: on_device(): lax.all_to_all(local, 'shard', split_axis=0, concat_axis=1, tiled=True)]
    convert_element_type x1 -> x0, other arithmetic: 23.2 us -> none  [on_device(): fresh = new_global.astype(jnp.bfloat16)]
    sub x0 -> x1, other arithmetic: none -> 22.8 us  [on_device(): global_weights - outer_rate * (delta + momentum_decay * new_momentum)]
    all_gather x1 -> x0, local copies, waits for them, and re-layouts: 14.7 us -> none  [on_device(): lax.all_gather(spread.reshape(shards, 1, owned, width), 'rep', axis=1, ti...]
  transfers between devices with their start and end apart: 2 -> 0, of which waited for: 0 -> 0; matrix products, arithmetic and copies ran while one was open for 10% -> 0% of each run, Pallas kernels for 0% -> 0%
where the time goes in v1:
time: 353 us
  Pallas kernels  320 us (91%)
  other arithmetic  22.8 us (6%)
  local copies, waits for them, and re-layouts  8.77 us (2%)
    pallas_call x1, Pallas kernels, by_kernel(): pl.pallas_call(functools.partial(exchange, n, pairs), out_shape=(jax.Shap...  320 us
    sub x1, other arithmetic, on_device(): global_weights - outer_rate * (delta + momentum_decay * new_momentum)  22.8 us
    unnamed x3, local copies, waits for them, and re-layouts  8.77 us

profile of v1, /device:TPU:10, one launch (start us, length us, event | category | flops | bytes accessed | tf_op | source)
XLA Modules:
  0.0 352.6 jit_solution(12743988580260958914)
XLA Ops:
  0.6 320.4 %shard_map.58 = (bf16[256,14336]{1,0:T(8,128)(2,1)}, bf16[4096,1792]{1,0:T(8,128)(2,1)}) custom-call(bf16[4096,1792]{1,0:T(8,128)(2,1)} %bitcast.1, f32[256,14336]{1,0:T(8,128)} %g_ref.1, f32[256,14336]{1,0:T(8,128)} %m_ref.1), custom_call_target="tpu_custom_call" | custom-call | tf_op jit(solution)/shard_map/pallas_call | solution.py:148
  321.0 0.0 copy-start
  321.0 22.8 %multiply_subtract_fusion = (f32[256,14336]{1,0:T(8,128)}, f32[256,14336]{1,0:T(8,128)}) fusion(f32[256,14336]{1,0:T(8,128)} %g_ref.1, bf16[256,14336]{1,0:T(8,128)(2,1)} %get-tuple-element.6, f32[256,14336]{1,0:T(8,128)} %m_ref.1), kind=kLoop, calls=%fused_computation | loop fusion | flops 33030144 | bytes 66060288 | tf_op jit(solution)/shard_map/sub | solution.py:185
  343.8 3.3 copy-done
  347.1 5.5 %copy.7 = bf16[4096,1792]{1,0:T(8,128)(2,1)} copy(bf16[4096,1792]{1,0:T(8,128)(2,1)S(1)} %copy-done) | data formatting | bytes 29360128
Async XLA Ops:
  321.0 26.1 %copy-start = (bf16[4096,1792]{1,0:T(8,128)(2,1)S(1)}, bf16[4096,1792]{1,0:T(8,128)(2,1)}, u32[]{:S(2)}) copy-start(bf16[4096,1792]{1,0:T(8,128)(2,1)} %get-tuple-element.12) | copy-start | bytes 44040196

commit v2 on v1

--- a/solution.py
+++ b/solution.py
@@ -13,8 +13,9 @@
 CHUNK = 16
 
 
-def far_first(n):
-    return sorted(range(1, n), key=lambda k: abs(2 * k - n)) + [0]
+def mixed(n):
+    far = sorted(range(1, n), key=lambda k: abs(2 * k - n))
+    return [far[j // 2] if j % 2 == 0 else far[-1 - j // 2] for j in range(n - 1)] + [0]
 
 
 def exchange(n, pairs, w_ref, g_ref, m_ref, t_ref, p_ref, peer_w, tot, q_out, q_in,
@@ -23,7 +24,7 @@
     me, rep = lax.axis_index("shard"), lax.axis_index("rep")
     other = 1 - rep
     owned, width = g_buf.shape[1:]
-    steps = far_first(n)
+    steps = mixed(n)
     on_total = outer_rate * (1 + momentum_decay) / pairs
     on_global = 1 - outer_rate * (1 + momentum_decay)
     on_momentum = -outer_rate * momentum_decay * momentum_decay

time: 353 us -> 353 us (level)
  no operation moved by 1% of the time
where the time goes in v2:
time: 353 us; the launch traced here: 352 us
  Pallas kernels  320 us (91%)
  other arithmetic  22.8 us (6%)
  local copies, waits for them, and re-layouts  8.77 us (2%)
    pallas_call x1, Pallas kernels, by_kernel(): pl.pallas_call(functools.partial(exchange, n, pairs), out_shape=(jax.Shap...  320 us
    sub x1, other arithmetic, on_device(): global_weights - outer_rate * (delta + momentum_decay * new_momentum)  22.8 us
    unnamed x3, local copies, waits for them, and re-layouts  8.77 us

profile of v2, /device:TPU:10, one launch (start us, length us, event | category | flops | bytes accessed | tf_op | source)
XLA Modules:
  0.0 352.4 jit_solution(11911730744354099043)
XLA Ops:
  0.6 320.3 %shard_map.58 = (bf16[256,14336]{1,0:T(8,128)(2,1)}, bf16[4096,1792]{1,0:T(8,128)(2,1)}) custom-call(bf16[4096,1792]{1,0:T(8,128)(2,1)} %bitcast.1, f32[256,14336]{1,0:T(8,128)} %g_ref.1, f32[256,14336]{1,0:T(8,128)} %m_ref.1), custom_call_target="tpu_custom_call" | custom-call | tf_op jit(solution)/shard_map/pallas_call | solution.py:149
  320.9 0.0 copy-start
  320.9 22.8 %multiply_subtract_fusion = (f32[256,14336]{1,0:T(8,128)}, f32[256,14336]{1,0:T(8,128)}) fusion(f32[256,14336]{1,0:T(8,128)} %g_ref.1, bf16[256,14336]{1,0:T(8,128)(2,1)} %get-tuple-element.6, f32[256,14336]{1,0:T(8,128)} %m_ref.1), kind=kLoop, calls=%fused_computation | loop fusion | flops 33030144 | bytes 66060288 | tf_op jit(solution)/shard_map/sub | solution.py:186
  343.7 3.3 copy-done
  347.0 5.5 %copy.7 = bf16[4096,1792]{1,0:T(8,128)(2,1)} copy(bf16[4096,1792]{1,0:T(8,128)(2,1)S(1)} %copy-done) | data formatting | bytes 29360128
Async XLA Ops:
  320.9 26.1 %copy-start = (bf16[4096,1792]{1,0:T(8,128)(2,1)S(1)}, bf16[4096,1792]{1,0:T(8,128)(2,1)}, u32[]{:S(2)}) copy-start(bf16[4096,1792]{1,0:T(8,128)(2,1)} %get-tuple-element.12) | copy-start | bytes 44040196
